TPU v7x, 256 devices: a whole 4x4x8 slice. The times are simulated.
256 devices in a mesh: mode: 64 (over y, z, core), row: 4 (over x).
Axes of the slice: x: 4, y: 4, z: 8, core: 2. Of those that a mesh axis runs over, the one named last changes fastest.
Arguments:
- density: float32 [2, 2048, 2048], P(None, 'row', 'mode'), may hold values from -6 to 6
- auxiliary: float32 [2048, 256, 2, 128], P('row', 'mode'), may hold values from -2 to 2
- hamiltonian: bfloat16 [2048, 2048], P('row'), as said below
- coupling: int32 [2, 128], replicated, may hold values from 0 to 2047, as said below
- lead_index: int32 [256], P('mode'), may hold values from 0 to 1
- mode_level: float32 [256], P('mode'), may hold values from -2 to 2
- mode_width: float32 [256], P('mode'), may hold values from 0.05 to 3
- residue: float32 [256, 2], P('mode'), may hold values from -4 to 4
- occupation: float32 [256], P('mode'), may hold values from 0 to 1
- lead_gamma: bfloat16 [2, 128, 128], replicated, may hold values from -0.5 to 0.5
Outputs:
- density_rate: float32 [2, 2048, 2048], P(None, 'row', 'mode')
- auxiliary_rate: float32 [2048, 256, 2, 128], P('row', 'mode')
Inputs may be any that keep to these rules, and one draw needn't show every extreme that they name: `coupling`: all 256 entries are distinct orbitals. `hamiltonian`: Symmetric.
All inputs are finite; a program needn't handle non-finite values.
Results may differ from a plain program's by a relative error of at most 0.0044.
Values may be sent and summed in bfloat16 or wider, within the bound.
A program may use at most 128 MiB of HBM per device.

v0:
```python
import jax
import jax.numpy as jnp
from jax import lax
from jax.sharding import PartitionSpec as P

H2 = 0.05
F32 = jnp.float32
BF = jnp.bfloat16


def dot(a, b, ca=1, cb=0):
    return lax.dot_general(a, b, (((ca,), (cb,)), ((), ())), preferred_element_type=F32)


def over_row(x):
    devices = lax.axis_size("row")
    return lax.all_to_all(jnp.broadcast_to(x[None], (devices, *x.shape)), "row", 0, 0, tiled=True)


def by_lead(x, gamma):
    leads, coupled = gamma.shape[:2]
    return jnp.concatenate(
        [dot(x[:, l * coupled : (l + 1) * coupled], gamma[l]) for l in range(leads)], axis=1
    )


def shards(
    density,
    auxiliary,
    hamiltonian,
    coupling,
    lead_index,
    mode_level,
    mode_width,
    residue,
    occupation,
    lead_gamma,
):
    rows, cols = density.shape[1:]
    n = hamiltonian.shape[1]
    leads, coupled = coupling.shape
    q = leads * coupled
    modes = auxiliary.shape[1]
    n_mode = lax.axis_size("mode")
    n_row = lax.axis_size("row")
    x_pos, m_pos = (lax.axis_index("row"), lax.axis_index("mode"))
    row_start, col_start = (x_pos * rows, m_pos * cols)
    flat = coupling.reshape(-1)
    e_full = (jnp.arange(n, dtype=jnp.int32)[:, None] == flat[None, :]).astype(BF)
    e_row = (row_start + jnp.arange(rows, dtype=jnp.int32)[:, None] == flat[None, :]).astype(BF)
    e_col = (col_start + jnp.arange(cols, dtype=jnp.int32)[:, None] == flat[None, :]).astype(BF)
    g_row = by_lead(e_row, lead_gamma).astype(BF)
    g_col = by_lead(e_col, lead_gamma).astype(BF)
    rho_t = jnp.swapaxes(density, 1, 2).astype(BF).reshape(2 * cols, rows)
    ham_ct = jnp.swapaxes(lax.dynamic_slice_in_dim(hamiltonian, col_start, cols, 1), 0, 1)
    first = over_row(jnp.concatenate([ham_ct, rho_t], axis=0))
    first = jnp.moveaxis(first, 0, 1).reshape(3 * cols, n)
    ham_c = first[:cols]
    applied = dot(first, hamiltonian, 1, 1)
    ham2_ct = applied[:cols].astype(BF)
    hrho_t = applied[cols:]
    he_row = dot(hamiltonian, e_full)
    hg_row = by_lead(he_row.astype(BF), lead_gamma)
    he_col = dot(ham_c, e_full).astype(BF)
    hg_col = by_lead(he_col, lead_gamma)
    panel = lax.all_gather(rho_t.reshape(2, cols, rows), "mode", axis=1, tiled=True)
    ham2_all = lax.all_gather(ham2_ct, "mode", axis=0, tiled=True)
    pi_b = auxiliary.astype(BF).reshape(rows, modes * 2 * coupled)
    pi_all = lax.all_gather(pi_b, "row", axis=0, tiled=True)
    onehot = (lead_index[:, None] == jnp.arange(leads, dtype=jnp.int32)[None, :]).astype(F32)
    lam_re, lam_im = (-mode_width, mode_level)
    l_parts, m_parts = ([[], []], [[], []])
    for l in range(leads):
        s = [sum((onehot[k, l] * auxiliary[:, k, p] for k in range(modes))) for p in range(2)]
        m_re = sum(
            (
                onehot[k, l] * (lam_re[k] * auxiliary[:, k, 0] - lam_im[k] * auxiliary[:, k, 1])
                for k in range(modes)
            )
        )
        m_im = sum(
            (
                onehot[k, l] * (lam_re[k] * auxiliary[:, k, 1] + lam_im[k] * auxiliary[:, k, 0])
                for k in range(modes)
            )
        )
        for p in range(2):
            l_parts[p].append(s[p])
        m_parts[0].append(m_re)
        m_parts[1].append(m_im)
    l_part = jnp.concatenate(l_parts[0] + l_parts[1], axis=1)
    m_part = jnp.concatenate(m_parts[0] + m_parts[1], axis=1)
    w_l = jnp.concatenate([(residue[:, p][:, None] * onehot).sum(0) for p in range(2)])
    v_l = jnp.concatenate(
        [((residue[:, p] * occupation)[:, None] * onehot).sum(0) for p in range(2)]
    )
    hrho_b = hrho_t.astype(BF)
    f_re = dot(
        jnp.concatenate([hrho_b[cols:], rho_t[cols:]], 0),
        jnp.concatenate([2 * g_col, -hg_col.astype(BF)], 0),
        0,
        0,
    )
    f_im = dot(
        jnp.concatenate([hrho_b[:cols], rho_t[:cols]], 0),
        jnp.concatenate([-2 * g_col, hg_col.astype(BF)], 0),
        0,
        0,
    )
    f_part = jnp.concatenate([f_re, f_im], axis=1)
    l_part_b = l_part.astype(BF)
    n_part = jnp.concatenate(
        [dot(l_part_b[:, :q], g_row, 0, 0), -dot(l_part_b[:, q:], g_row, 0, 0)], axis=1
    )
    piece = rows // n_mode
    n_piece = q // n_mode
    scal = jnp.concatenate([w_l, v_l])
    scal = jnp.zeros((n_mode, 1, 2 * q), F32).at[:, 0, : scal.shape[0]].set(scal)
    payload = jnp.concatenate(
        [a.reshape(n_mode, -1, 2 * q) for a in (l_part, m_part, f_part, n_part)] + [scal], axis=1
    )
    mine = lax.psum_scatter(payload, "mode", scatter_dimension=0, tiled=True)[0]
    n_mine = over_row(mine[3 * piece : 3 * piece + n_piece]).sum(0)
    w_sum, v_sum = (mine[-1, : 2 * leads], mine[-1, 2 * leads : 4 * leads])
    mine = jnp.concatenate([mine[: 3 * piece], n_mine], axis=0).astype(BF)
    whole = lax.all_gather(mine, "mode", axis=0, tiled=False)
    l1_b = whole[:, :piece].reshape(rows, 2 * q)
    m1 = whole[:, piece : 2 * piece].reshape(rows, 2 * q).astype(F32)
    f_all = whole[:, 2 * piece : 3 * piece].reshape(rows, 2 * q).astype(F32)
    n_all = whole[:, 3 * piece :].reshape(q, 2 * q)
    grow_full = by_lead(e_full, lead_gamma).astype(BF)
    src = jnp.concatenate([dot(panel[p], grow_full, 0, 0) for p in range(2)], axis=1)
    w_q = jnp.repeat(w_sum, coupled)
    v_q = jnp.repeat(v_sum, coupled)
    s_re, s_im = (src[:, :q], src[:, q:])
    g_row_f = g_row.astype(F32)
    drive = jnp.concatenate(
        [
            w_q[:q] * s_re - w_q[q:] * s_im - (v_q[:q] - v_q[q:]) * g_row_f,
            w_q[:q] * s_im + w_q[q:] * s_re - (v_q[:q] + v_q[q:]) * g_row_f,
        ],
        axis=1,
    )
    x_row = (3.0 * l1_b.astype(F32) + 2 * H2 * (m1 + drive)).astype(BF)
    p1 = jnp.concatenate([dot(e_col, l1_b[:, p * q : (p + 1) * q], 1, 1) for p in range(2)], 0)
    xe = jnp.concatenate([dot(e_col, x_row[:, p * q : (p + 1) * q], 1, 1) for p in range(2)], 0)
    rhoh_t = jnp.concatenate([dot(ham_c, panel[p]) for p in range(2)], 0)
    y = hrho_t - 2.0 * rhoh_t + 2.0 * jnp.concatenate([-p1[cols:], p1[:cols]], 0)
    z = dot(lax.dynamic_slice_in_dim(ham_c, row_start, rows, 1), l1_b)
    owner = col_start // rows
    own_l = lax.dynamic_slice_in_dim(l1_b, col_start - owner * rows, cols, 0)
    own_x = lax.dynamic_slice_in_dim(x_row, col_start - owner * rows, cols, 0)
    mask = (x_pos == owner).astype(BF)
    second = over_row(jnp.concatenate([y.astype(BF), ham2_ct], 0))
    second = jnp.moveaxis(second, 0, 1).reshape(3 * cols, n)
    third = (
        over_row(jnp.concatenate([z.astype(BF), own_l * mask, own_x * mask], 0)).astype(F32).sum(0)
    )
    z, l_c, x_c = (third[:cols], third[cols : 2 * cols], third[2 * cols :])
    hy = dot(second[: 2 * cols], hamiltonian, 1, 1)
    ham2_c = second[2 * cols :]
    rhoh2_t = jnp.concatenate([dot(ham2_c, panel[p]) for p in range(2)], 0)
    b_re = x_c[:, :q] + 4 * H2 * z[:, q:]
    b_im = -x_c[:, q:] + 4 * H2 * z[:, :q]
    back_re = dot(b_re.astype(BF), e_row, 1, 1)
    back_im = dot(b_im.astype(BF), e_row, 1, 1)
    l_cb = l_c.astype(BF)
    he_row_b = he_row.astype(BF)
    c1_re, c1_im = (dot(l_cb[:, :q], he_row_b, 1, 1), -dot(l_cb[:, q:], he_row_b, 1, 1))
    c2_re, c2_im = (dot(he_col, l1_b[:, :q], 1, 1), dot(he_col, l1_b[:, q:], 1, 1))
    d_re, d_im = (c1_re - c2_re, c1_im - c2_im)
    comm = hrho_t - rhoh_t
    base = -2 * H2 * (hy + rhoh2_t) + xe
    out_re = 3.0 * comm[cols:] + base[:cols] + back_re + 2 * H2 * d_im
    out_im = -3.0 * comm[:cols] + base[cols:] + back_im - 2 * H2 * d_re
    density_rate = jnp.swapaxes(jnp.stack([out_re, out_im]), 1, 2)
    h_pi = dot(hamiltonian, pi_all).reshape(rows, modes, 2, coupled)
    h2_pi = dot(ham2_all, pi_all.reshape(n, -1), 0, 0).reshape(rows, modes, 2, coupled)
    lg = jnp.concatenate([by_lead(l1_b[:, p * q : (p + 1) * q], lead_gamma) for p in range(2)], 1)
    u = 2 * H2 * (f_all + lg + dot(e_row, n_all))
    outs = []
    for k in range(modes):
        is0 = onehot[k, 0] > 0

        def pick(a):
            return jnp.where(is0, a[:, :coupled], a[:, coupled:])

        lr, li = (lam_re[k], lam_im[k])
        wr, wi, occ = (residue[k, 0], residue[k, 1], occupation[k])
        sr, si, ur, ui = (pick(s_re), pick(s_im), pick(u[:, :q]), pick(u[:, q:]))
        gk, hgk = (pick(g_row_f), pick(hg_row))
        br, bi = (sr - occ * gk, si - occ * gk)
        ar, ai = (3 + 2 * H2 * lr, 2 * H2 * li)
        tr = ar * br - ai * bi + ur - 2 * H2 * occ * hgk
        ti = ar * bi + ai * br + ui + 2 * H2 * occ * hgk
        pr, pim = (auxiliary[:, k, 0], auxiliary[:, k, 1])
        cr = 3 * lr + 2 * H2 * (lr * lr - li * li)
        ci = 3 * li + 4 * H2 * lr * li
        er, ei = (4 * H2 * li, -3 - 4 * H2 * lr)
        hr, hi = (h_pi[:, k, 0], h_pi[:, k, 1])
        outs.append(
            cr * pr - ci * pim + er * hr - ei * hi - 2 * H2 * h2_pi[:, k, 0] + wr * tr - wi * ti
        )
        outs.append(
            cr * pim + ci * pr + er * hi + ei * hr - 2 * H2 * h2_pi[:, k, 1] + wr * ti + wi * tr
        )
    auxiliary_rate = jnp.stack(outs, axis=1).reshape(rows, modes, 2, coupled)
    return (density_rate, auxiliary_rate)


def solution(mesh):
    in_specs = (
        P(None, "row", "mode"),
        P("row", "mode", None, None),
        P("row", None),
        P(),
        P("mode"),
        P("mode"),
        P("mode"),
        P("mode", None),
        P("mode"),
        P(),
    )
    out_specs = (P(None, "row", "mode"), P("row", "mode", None, None))
    return jax.shard_map(shards, mesh=mesh, in_specs=in_specs, out_specs=out_specs, check_vma=False)
```

profile of v0, /device:TPU:1, one launch (start us, length us, event | category | flops | bytes accessed | tf_op | source)
XLA Modules:
  0.0 596.0 jit_solution(17959333989548009049)
XLA Ops:
  9.8 4.8 all-to-all-start
  14.7 4.1 fusion.164
  21.0 6.2 %convert_bitcast_fusion.1 = (bf16[512,128]{1,0:T(8,128)(2,1)}, f32[512,1,1,128]{3,0,2,1:T(8,128)}, bf16[512,128]{1,0:T(8,128)(2,1)}, f32[512,1,1,128]{3,0,2,1:T(...) fusion(f32[512,1,1,128]{3,0,2,1:T(8,128)S(1)} %bitcast.292, ...), kind=kLoop, calls=%fused_computation.175 | loop fusion | flops 2097152 | bytes 3670048 | tf_op jit(solution)/shard_map/add | solution.py:74
  27.2 8.4 %add_bitcast_fusion = f32[64,8,128]{2,1,0:T(8,128)} fusion(f32[]{:T(128)} %bitcast.15, f32[]{:T(128)} %bitcast.14, f32[]{:T(128)} %bitcast.13, f32[]{:T(128)} %bitcast.12, f32[512,1,1,128]{3,0,2,1:T(8,128)S(1)} %bitcast.272, f32[]{:T(128)} %bitcast.20, f32[512,1,1,128]{3,0,2,1:T(8,128)S(1)} %bitcast.279, f32[]{:T(128)} %bitcast.19, ...), kind=kLoop, calls=%fused_computation.101 | loop fusion | flops 1245184 | bytes 2359344 | tf_op jit(solution)/shard_map/add | solution.py:81
  35.6 8.4 %add_bitcast_fusion.1 = f32[64,8,128]{2,1,0:T(8,128)} fusion(f32[]{:T(128)} %bitcast.10, f32[]{:T(128)} %bitcast.9, f32[]{:T(128)} %bitcast.8, f32[]{:T(128)} %bitcast.7, f32[512,1,1,128]{3,0,2,1:T(8,128)S(1)} %bitcast.273, f32[]{:T(128)} %bitcast.20, f32[512,1,1,128]{3,0,2,1:T(8,128)S(1)} %bitcast.280, f32[]{:T(128)} %bitcast.19, ...), kind=kLoop, calls=%fused_computation.102 | loop fusion | flops 1245184 | bytes 2359344 | tf_op jit(solution)/shard_map/add | solution.py:81
  44.1 8.5 %add_bitcast_fusion.2 = f32[64,8,128]{2,1,0:T(8,128)} fusion(f32[]{:T(128)} %bitcast.15, f32[]{:T(128)} %bitcast.14, f32[]{:T(128)} %bitcast.13, f32[]{:T(128)} %bitcast.12, f32[512,1,1,128]{3,0,2,1:T(8,128)S(1)} %bitcast.281, f32[]{:T(128)} %bitcast.20, f32[512,1,1,128]{3,0,2,1:T(8,128)S(1)} %bitcast.274, f32[]{:T(128)} %bitcast.19, ...), kind=kLoop, calls=%fused_computation.103 | loop fusion | flops 1245184 | bytes 2359344 | tf_op jit(solution)/shard_map/add | solution.py:75
  52.6 8.4 %add_bitcast_fusion.3 = f32[64,8,128]{2,1,0:T(8,128)} fusion(f32[]{:T(128)} %bitcast.10, f32[]{:T(128)} %bitcast.9, f32[]{:T(128)} %bitcast.8, f32[]{:T(128)} %bitcast.7, f32[512,1,1,128]{3,0,2,1:T(8,128)S(1)} %bitcast.282, f32[]{:T(128)} %bitcast.20, f32[512,1,1,128]{3,0,2,1:T(8,128)S(1)} %bitcast.275, f32[]{:T(128)} %bitcast.19, ...), kind=kLoop, calls=%fused_computation.104 | loop fusion | flops 1245184 | bytes 2359344 | tf_op jit(solution)/shard_map/add | solution.py:75
  84.1 13.7 %concatenate.113 = f32[64,29,512]{2,1,0:T(8,128)} concatenate(f32[64,8,512]{2,1,0:T(8,128)} %pad_maximum_fusion, f32[64,8,512]{2,1,0:T(8,128)} %pad_maximum_fusion.1, f32[64,8,512]{2,1,0:T(8,128)} %bitcast.327, f32[64,4,512]{2,1,0:T(4,128)} %reshape.500, f32[64,1,512]{2,1,0:T(1,128)} %scatter.8), dimensions={1} | concatenate | bytes 7602176 | tf_op jit(solution)/shard_map/concatenate | solution.py:119
  99.4 3.3 convert_element_type.100
  144.5 96.6 %reduce-scatter.2.cloned.1.call-done = f32[1,29,512]{2,1,0:T(8,128)} async-done(((f32[64,29,512]{2,1,0:T(8,128)}), f32[1,29,512]{2,1,0:T(8,128)}) %reduce-scatter.2.cloned.1.call-update) | async-done | bytes 59408 | tf_op jit(solution)/shard_map/reduce_scatter | solution.py:122
  242.4 3.8 all-to-all-start.1
  251.2 74.0 %all-gather.11.cloned.1.call-done = bf16[2048,512]{1,0:T(8,128)(2,1)} async-done(((bf16[32,512]{1,0:T(8,128)(2,1)}), bf16[2048,512]{1,0:T(8,128)(2,1)}) %all-gather.11.cloned.1.call-update) | async-done | bytes 2097168 | tf_op jit(solution)/shard_map/all_gather | solution.py:67
  325.2 49.4 %all-gather.9.cloned.1.call-done = bf16[2048,1024]{1,0:T(8,128)(2,1)} async-done(((bf16[512,1024]{1,0:T(8,128)(2,1)}), bf16[2048,1024]{1,0:T(8,128)(2,1)}) %all-gather.9.cloned.1.call-update) | async-done | bytes 4194320 | tf_op jit(solution)/shard_map/all_gather | solution.py:69
  374.6 5.2 fusion.173
  383.0 4.6 fusion.172
  415.8 41.6 %all-gather.5.cloned.1.call-done = bf16[2,2048,512]{2,1,0:T(8,128)(2,1)} async-done(((bf16[2,32,512]{2,1,0:T(8,128)(2,1)}), bf16[2,2048,512]{2,1,0:T(8,128)(2,1)}) %all-gather.5.cloned.1.call-update) | async-done | bytes 4194320 | tf_op jit(solution)/shard_map/all_gather | solution.py:66
  457.5 3.0 fusion.8
  460.5 2.8 select_subtract_fusion.1
  465.3 2.8 select_subtract_fusion
  471.8 62.8 %all-gather.7.cloned.1.call-done = bf16[64,28,512]{2,1,0:T(8,128)(2,1)} async-done(((bf16[1,28,512]{2,1,0:T(8,128)(2,1)}), bf16[64,28,512]{2,1,0:T(8,128)(2,1)}) %all-gather.7.cloned.1.call-update) | async-done | bytes 1835024 | tf_op jit(solution)/shard_map/all_gather | solution.py:126
  544.3 4.3 all-to-all-start.2
  566.6 2.9 copy.232
  572.5 4.0 all-to-all-start.3
  579.1 4.3 all-to-all-done.3
  (330 shorter events, 122.5 us)
Async XLA Ops:
  9.8 65.5 %all-to-all-start = ((bf16[4,96,512]{2,1,0:T(8,128)(2,1)}), bf16[4,96,512]{2,1,0:T(8,128)(2,1)}, u32[]{:S(2)}, u32[]{:S(2)}) async-start(bf16[4,96,512]{2,1,0:T(8,128)(2,1)} %broadcast_in_dim.18), calls=%async_computation | async-start | bytes 786432 | tf_op jit(solution)/shard_map/all_to_all | solution.py:17
  14.6 226.4 %reduce-scatter.2.cloned.1.call-start = ((), (), s32[]{:S(2)}) async-start(), calls=%async_computation.6 | async-start | bytes 4259840 | tf_op jit(solution)/shard_map/reduce_scatter | solution.py:122
  14.7 60.0 %copy-start.48 = (bf16[2,32,512]{2,1,0:T(8,128)(2,1)}, bf16[2,32,512]{2,1,0:T(8,128)(2,1)S(1)}, u32[]{:S(2)}) copy-start(bf16[2,32,512]{2,1,0:T(8,128)(2,1)S(1)} %convert_bitcast_fusion.5) | copy-start | bytes 196612
  18.8 33.8 %copy-start.1 = (f32[512,1,1,128]{3,2,1,0:T(1,128)}, f32[512,1,1,128]{3,2,1,0:T(1,128)S(1)}, u32[]{:S(2)}) copy-start(f32[512,1,1,128]{3,2,1,0:T(1,128)S(1)} %get-tuple-element.71) | copy-start | bytes 786436
  18.8 33.8 %copy-start.3 = (f32[512,1,1,128]{3,2,1,0:T(1,128)}, f32[512,1,1,128]{3,2,1,0:T(1,128)S(1)}, u32[]{:S(2)}) copy-start(f32[512,1,1,128]{3,2,1,0:T(1,128)S(1)} %get-tuple-element.68) | copy-start | bytes 786436
  18.8 33.7 %copy-start.5 = (f32[512,1,1,128]{3,2,1,0:T(1,128)}, f32[512,1,1,128]{3,2,1,0:T(1,128)S(1)}, u32[]{:S(2)}) copy-start(f32[512,1,1,128]{3,2,1,0:T(1,128)S(1)} %get-tuple-element.72) | copy-start | bytes 786436
  44.1 17.4 %copy-start.65 = (s32[2,128]{1,0:T(2,128)S(1)}, s32[2,128]{1,0:T(2,128)}, u32[]{:S(2)}) copy-start(s32[2,128]{1,0:T(2,128)} %param.15) | copy-start | bytes 3076
  44.1 17.5 %copy-start.24 = (bf16[2,128,128]{2,1,0:T(8,128)(2,1)S(1)}, bf16[2,128,128]{2,1,0:T(8,128)(2,1)}, u32[]{:S(2)}) copy-start(bf16[2,128,128]{2,1,0:T(8,128)(2,1)} %param.21) | copy-start | bytes 196612
  97.8 227.4 %all-gather.11.cloned.1.call-start = ((), (), s32[]{:S(2)}) async-start(), calls=%async_computation.9 | async-start | bytes 2129920 | tf_op jit(solution)/shard_map/all_gather | solution.py:67
  99.3 275.3 %all-gather.9.cloned.1.call-start = ((), (), s32[]{:S(2)}) async-start(), calls=%async_computation.8 | async-start | bytes 5242880 | tf_op jit(solution)/shard_map/all_gather | solution.py:69
  105.2 352.2 %all-gather.5.cloned.1.call-start = ((), (), s32[]{:S(2)}) async-start(), calls=%async_computation.5 | async-start | bytes 4259840 | tf_op jit(solution)/shard_map/all_gather | solution.py:66
  242.4 8.1 %all-to-all-start.1 = ((f32[4,4,512]{2,1,0:T(4,128)}), f32[4,4,512]{2,1,0:T(4,128)S(1)}, u32[]{:S(2)}, u32[]{:S(2)}) async-start(f32[4,4,512]{2,1,0:T(4,128)} %broadcast_in_dim.20), calls=%async_computation.2 | async-start | bytes 65536 | tf_op jit(solution)/shard_map/all_to_all | solution.py:17
  246.2 288.4 %all-gather.7.cloned.1.call-start = ((), (), s32[]{:S(2)}) async-start(), calls=%async_computation.7 | async-start | bytes 2129920 | tf_op jit(solution)/shard_map/all_gather | solution.py:126
  415.8 47.4 %copy-start.86 = (f32[256]{0:T(256)S(1)}, f32[256]{0:T(256)}, u32[]{:S(2)}) copy-start(f32[256]{0:T(256)} %broadcast_bitcast_fusion.1) | copy-start | bytes 3076
  415.8 47.4 %copy-start.87 = (f32[256]{0:T(256)S(1)}, f32[256]{0:T(256)}, u32[]{:S(2)}) copy-start(f32[256]{0:T(256)} %broadcast_bitcast_fusion.2) | copy-start | bytes 3076
  415.8 47.4 %copy-start.88 = (f32[256]{0:T(256)S(1)}, f32[256]{0:T(256)}, u32[]{:S(2)}) copy-start(f32[256]{0:T(256)} %broadcast_bitcast_fusion.3) | copy-start | bytes 3076
  415.8 47.4 %copy-start.89 = (f32[256]{0:T(256)S(1)}, f32[256]{0:T(256)}, u32[]{:S(2)}) copy-start(f32[256]{0:T(256)} %broadcast_bitcast_fusion) | copy-start | bytes 3076
  470.7 65.1 %copy-start.78 = (s32[32]{0:T(128)S(1)}, s32[32]{0:T(128)}, u32[]{:S(2)}) copy-start(s32[32]{0:T(128)} %copy-done.77) | copy-start | bytes 388
  471.8 66.7 %copy-start.66 = (s32[2,128]{1,0:T(2,128)S(1)}, s32[2,128]{1,0:T(2,128)}, u32[]{:S(2)}) copy-start(s32[2,128]{1,0:T(2,128)} %param.15) | copy-start | bytes 3076
  540.2 12.0 %copy-start.73 = (s32[512]{0:T(512)S(1)}, s32[512]{0:T(512)}, u32[]{:S(2)}) copy-start(s32[512]{0:T(512)} %copy-done.72) | copy-start | bytes 6148
  544.3 27.4 %all-to-all-start.2 = ((bf16[4,96,512]{2,1,0:T(8,128)(2,1)}), bf16[4,96,512]{2,1,0:T(8,128)(2,1)}, u32[]{:S(2)}, u32[]{:S(2)}) async-start(bf16[4,96,512]{2,1,0:T(8,128)(2,1)} %broadcast_in_dim.21), calls=%async_computation.3 | async-start | bytes 786432 | tf_op jit(solution)/shard_map/all_to_all | solution.py:17
  569.5 13.9 %copy-start.15 = (bf16[256,512]{1,0:T(8,128)(2,1)S(1)}, bf16[256,512]{1,0:T(8,128)(2,1)}, u32[]{:S(2)}) copy-start(bf16[256,512]{1,0:T(8,128)(2,1)} %copy-done.13) | copy-start | bytes 786436
  570.9 12.9 %copy-start.8 = (bf16[512,512]{1,0:T(8,128)(2,1)S(1)}, bf16[512,512]{1,0:T(8,128)(2,1)}, u32[]{:S(2)}) copy-start(bf16[512,512]{1,0:T(8,128)(2,1)} %copy-done.7) | copy-start | bytes 1572868
  572.5 10.8 %all-to-all-start.3 = ((bf16[4,96,512]{2,1,0:T(8,128)(2,1)}), bf16[4,96,512]{2,1,0:T(8,128)(2,1)S(1)}, u32[]{:S(2)}, u32[]{:S(2)}) async-start(bf16[4,96,512]{2,1,0:T(8,128)(2,1)} %broadcast_in_dim.26), calls=%async_computation.4 | async-start | bytes 786432 | tf_op jit(solution)/shard_map/all_to_all | solution.py:17
  (77 other events, 231.3 us)
Sparse Core Ops, SparseCore 0:
  97.9 143.1 reduce-scatter.1
  243.9 81.2 all-gather.10
  327.0 47.5 all-gather.8
  377.3 80.1 all-gather.4
  460.1 74.4 all-gather.6
where the time goes:
time: 599 us; the launch traced here: 596 us
  waiting for transfers between devices  329 us (55%)
  local copies, waits for them, and re-layouts  86.9 us (15%)
  other arithmetic  74.6 us (12%)
  between operations  45.6 us (8%)
  matrix products  42.4 us (7%)
  starting transfers between devices  17.1 us (3%)
    reduce_scatter x1, waiting for transfers between devices, shards(): mine = lax.psum_scatter(payload, 'mode', scatter_dimension=0, tiled=True)[0]  96.6 us
    all_gather x1, waiting for transfers between devices, shards(): ham2_all = lax.all_gather(ham2_ct, 'mode', axis=0, tiled=True)  74 us
    all_gather x1, waiting for transfers between devices, shards(): whole = lax.all_gather(mine, 'mode', axis=0, tiled=False)  62.8 us
    all_gather x1, waiting for transfers between devices, shards(): pi_all = lax.all_gather(pi_b, 'row', axis=0, tiled=True)  49.4 us
    dot_general x42, matrix products, dot(): lax.dot_general(a, b, (((ca,), (cb,)), ((), ())), preferred_element_type=...  42.4 us
    all_gather x1, waiting for transfers between devices, shards(): lax.all_gather(rho_t.reshape(2, cols, rows), 'mode', axis=1, tiled=True)  41.6 us
    unnamed x204, local copies, waits for them, and re-layouts  38 us
    all_to_all x4, starting transfers between devices, over_row(): lax.all_to_all(jnp.broadcast_to(x[None], (devices, *x.shape)), 'row', 0,...  17 us
  transfers between devices with their start and end apart: 9, of which 6 were waited for; matrix products, arithmetic and copies ran while one was open for 27% of the time, Pallas kernels for 0%

commit v1 on v0

--- a/solution.py
+++ b/solution.py
@@ -6,6 +6,34 @@
 H2 = 0.05
 F32 = jnp.float32
 BF = jnp.bfloat16
+
+
+def spread_the_ends(xin, row_dim):
+    xin = jnp.moveaxis(xin, 0, row_dim)
+    lower = xin.shape
+    return xin.reshape(*lower[:row_dim], lower[row_dim] * lower[row_dim + 1], *lower[row_dim + 2 :])
+
+
+def edit_target_up(ax_name, inputs, axis_no=0):
+    size_here = lax.axis_size(ax_name)
+    slots = [(k0, (k0 + 1) % size_here) for k0 in range(size_here)]
+    arrivals = [(rr, h) for h, rr in slots]
+    r2, latest = ([], [])
+    c = 0
+    while c < size_here - 1:
+        if c % 2 == 0:
+            block_out = lax.ppermute(r2[-1] if r2 else inputs, ax_name, slots)
+            r2.append(block_out)
+        else:
+            mixed_arr = lax.ppermute(latest[-1] if latest else inputs, ax_name, arrivals)
+            latest.append(mixed_arr)
+        c += 1
+    f_next = jnp.stack([*r2[::-1], inputs, *latest])
+    current_value = lax.axis_index(ax_name)
+    big = len(r2)
+    a_next = current_value - big
+    f_next = f_next[(jnp.arange(size_here) - a_next) % size_here]
+    return spread_the_ends(f_next, axis_no)
 
 
 def dot(a, b, ca=1, cb=0):
@@ -66,7 +94,7 @@
     panel = lax.all_gather(rho_t.reshape(2, cols, rows), "mode", axis=1, tiled=True)
     ham2_all = lax.all_gather(ham2_ct, "mode", axis=0, tiled=True)
     pi_b = auxiliary.astype(BF).reshape(rows, modes * 2 * coupled)
-    pi_all = lax.all_gather(pi_b, "row", axis=0, tiled=True)
+    pi_all = edit_target_up("row", pi_b)
     onehot = (lead_index[:, None] == jnp.arange(leads, dtype=jnp.int32)[None, :]).astype(F32)
     lam_re, lam_im = (-mode_width, mode_level)
     l_parts, m_parts = ([[], []], [[], []])

time: 599 us -> 548 us (0.915)
  waiting for transfers between devices: 329 us -> 270 us
    all_gather x1 -> x0, waiting for transfers between devices: 49.4 us -> none  [shards(): pi_all = lax.all_gather(pi_b, 'row', axis=0, tiled=True)]
    reduce_scatter x1, waiting for transfers between devices: 96.6 us -> 56.9 us  [shards(): mine = lax.psum_scatter(payload, 'mode', scatter_dimension=0, tiled=True)[0]]
    all_gather x1, waiting for transfers between devices: 41.6 us -> 71.8 us  [shards(): lax.all_gather(rho_t.reshape(2, cols, rows), 'mode', axis=1, tiled=True)]
    all_gather x1, waiting for transfers between devices: 74 us -> 53.9 us  [shards(): ham2_all = lax.all_gather(ham2_ct, 'mode', axis=0, tiled=True)]
    ppermute x0 -> x3, waiting for transfers between devices: none -> 20.1 us  [the longest x2 20.1 us: edit_target_up(): block_out = lax.ppermute(r2[-1] if r2 else inputs, ax_name, slots)]
    unnamed x204 -> x174, local copies, waits for them, and re-layouts: 38 us -> 24.1 us
    reshape x0 -> x1, local copies, waits for them, and re-layouts: none -> 6.56 us  [spread_the_ends(): xin.reshape(*lower[:row_dim], lower[row_dim] * lower[row_dim + 1], *lower...]
  transfers between devices with their start and end apart: 9 -> 11, of which waited for: 6 -> 6; matrix products, arithmetic and copies ran while one was open for 27% -> 30% of each run, Pallas kernels for 0% -> 0%
where the time goes in v1:
time: 548 us; the launch traced here: 545 us
  waiting for transfers between devices  270 us (49%)
  local copies, waits for them, and re-layouts  85.2 us (16%)
  other arithmetic  78 us (14%)
  matrix products  46.1 us (8%)
  between operations  44.8 us (8%)
  starting transfers between devices  20.3 us (4%)
    all_gather x1, waiting for transfers between devices, shards(): lax.all_gather(rho_t.reshape(2, cols, rows), 'mode', axis=1, tiled=True)  71.8 us
    all_gather x1, waiting for transfers between devices, shards(): whole = lax.all_gather(mine, 'mode', axis=0, tiled=False)  62.6 us
    reduce_scatter x1, waiting for transfers between devices, shards(): mine = lax.psum_scatter(payload, 'mode', scatter_dimension=0, tiled=True)[0]  56.9 us
    all_gather x1, waiting for transfers between devices, shards(): ham2_all = lax.all_gather(ham2_ct, 'mode', axis=0, tiled=True)  53.9 us
    dot_general x42, matrix products, dot(): lax.dot_general(a, b, (((ca,), (cb,)), ((), ())), preferred_element_type=...  46.1 us
    unnamed x174, local copies, waits for them, and re-layouts  24.1 us
    ppermute x2, waiting for transfers between devices, edit_target_up(): block_out = lax.ppermute(r2[-1] if r2 else inputs, ax_name, slots)  20.1 us
    all_to_all x4, starting transfers between devices, over_row(): lax.all_to_all(jnp.broadcast_to(x[None], (devices, *x.shape)), 'row', 0,...  17.3 us
  transfers between devices with their start and end apart: 11, of which 6 were waited for; matrix products, arithmetic and copies ran while one was open for 30% of the time, Pallas kernels for 0%

profile of v1, /device:TPU:1, one launch (start us, length us, event | category | flops | bytes accessed | tf_op | source)
XLA Modules:
  0.0 544.9 jit_solution(5262180462119016234)
XLA Ops:
  9.8 4.8 all-to-all-start
  14.7 4.2 fusion.207
  21.2 6.2 %convert_bitcast_fusion.1 = (bf16[512,128]{1,0:T(8,128)(2,1)}, f32[512,1,1,128]{3,0,2,1:T(8,128)}, bf16[512,128]{1,0:T(8,128)(2,1)}, f32[512,1,1,128]{3,0,2,1:T(...) fusion(f32[512,1,1,128]{3,0,2,1:T(8,128)S(1)} %bitcast.356, ...), kind=kLoop, calls=%fused_computation.211 | loop fusion | flops 2097152 | bytes 3670048 | tf_op jit(solution)/shard_map/add | solution.py:102
  27.4 8.3 %add_bitcast_fusion = f32[64,8,128]{2,1,0:T(8,128)} fusion(f32[]{:T(128)} %bitcast.15, f32[]{:T(128)} %bitcast.14, f32[]{:T(128)} %bitcast.13, f32[]{:T(128)} %bitcast.12, f32[512,1,1,128]{3,0,2,1:T(8,128)S(1)} %bitcast.336, f32[]{:T(128)} %bitcast.20, f32[512,1,1,128]{3,0,2,1:T(8,128)S(1)} %bitcast.343, f32[]{:T(128)} %bitcast.19, ...), kind=kLoop, calls=%fused_computation.137 | loop fusion | flops 1245184 | bytes 2359344 | tf_op jit(solution)/shard_map/add | solution.py:109
  35.7 8.3 %add_bitcast_fusion.1 = f32[64,8,128]{2,1,0:T(8,128)} fusion(f32[]{:T(128)} %bitcast.10, f32[]{:T(128)} %bitcast.9, f32[]{:T(128)} %bitcast.8, f32[]{:T(128)} %bitcast.7, f32[512,1,1,128]{3,0,2,1:T(8,128)S(1)} %bitcast.337, f32[]{:T(128)} %bitcast.20, f32[512,1,1,128]{3,0,2,1:T(8,128)S(1)} %bitcast.344, f32[]{:T(128)} %bitcast.19, ...), kind=kLoop, calls=%fused_computation.138 | loop fusion | flops 1245184 | bytes 2359344 | tf_op jit(solution)/shard_map/add | solution.py:109
  44.1 8.4 %add_bitcast_fusion.2 = f32[64,8,128]{2,1,0:T(8,128)} fusion(f32[]{:T(128)} %bitcast.15, f32[]{:T(128)} %bitcast.14, f32[]{:T(128)} %bitcast.13, f32[]{:T(128)} %bitcast.12, f32[512,1,1,128]{3,0,2,1:T(8,128)S(1)} %bitcast.345, f32[]{:T(128)} %bitcast.20, f32[512,1,1,128]{3,0,2,1:T(8,128)S(1)} %bitcast.338, f32[]{:T(128)} %bitcast.19, ...), kind=kLoop, calls=%fused_computation.139 | loop fusion | flops 1245184 | bytes 2359344 | tf_op jit(solution)/shard_map/add | solution.py:103
  52.5 8.3 %add_bitcast_fusion.3 = f32[64,8,128]{2,1,0:T(8,128)} fusion(f32[]{:T(128)} %bitcast.10, f32[]{:T(128)} %bitcast.9, f32[]{:T(128)} %bitcast.8, f32[]{:T(128)} %bitcast.7, f32[512,1,1,128]{3,0,2,1:T(8,128)S(1)} %bitcast.346, f32[]{:T(128)} %bitcast.20, f32[512,1,1,128]{3,0,2,1:T(8,128)S(1)} %bitcast.339, f32[]{:T(128)} %bitcast.19, ...), kind=kLoop, calls=%fused_computation.140 | loop fusion | flops 1245184 | bytes 2359344 | tf_op jit(solution)/shard_map/add | solution.py:103
  84.1 13.6 %concatenate.113 = f32[64,29,512]{2,1,0:T(8,128)} concatenate(f32[64,8,512]{2,1,0:T(8,128)} %pad_maximum_fusion.1, f32[64,8,512]{2,1,0:T(8,128)} %pad_maximum_fusion.2, f32[64,8,512]{2,1,0:T(8,128)} %bitcast.391, f32[64,4,512]{2,1,0:T(4,128)} %reshape.551, f32[64,1,512]{2,1,0:T(1,128)} %scatter.8), dimensions={1} | concatenate | bytes 7602176 | tf_op jit(solution)/shard_map/concatenate | solution.py:147
  100.0 3.3 convert_element_type.100
  149.5 20.1 %collective-permute-done.1 = bf16[512,1024]{1,0:T(8,128)(2,1)S(1)} collective-permute-done((bf16[512,1024]{1,0:T(8,128)(2,1)}, bf16[512,1024]{1,0:T(8,128)(2,1)S(1)}, u32[]{:S(2)}, u32[]{:S(2)}) %collective-permute-start.1) | collective-permute-done | bytes 1048608 | tf_op jit(solution)/shard_map/ppermute | solution.py:25
  169.5 3.4 pad_maximum_fusion
  172.9 5.1 gather_fusion
  178.0 6.0 %fusion.215 = f32[1024,512]{1,0:T(8,128)} fusion(bf16[2048,1024]{1,0:T(8,128)(2,1)} %bitcast.333, bf16[512,2048]{1,0:T(8,128)(2,1)S(1)} %copy-done), kind=kOutput, calls=%fused_computation.361 | convolution fusion | flops 2147483648 | bytes 8388608 | tf_op jit(solution)/shard_map/dot_general | solution.py:40
  184.0 56.9 %reduce-scatter.2.cloned.1.call-done = f32[1,29,512]{2,1,0:T(8,128)} async-done(((f32[64,29,512]{2,1,0:T(8,128)}), f32[1,29,512]{2,1,0:T(8,128)}) %reduce-scatter.2.cloned.1.call-update) | async-done | bytes 59408 | tf_op jit(solution)/shard_map/reduce_scatter | solution.py:150
  242.2 4.0 all-to-all-start.1
  249.0 6.6 %copy.241 = bf16[2048,1024]{0,1:T(8,128)(2,1)} copy(bf16[2048,1024]{1,0:T(8,128)(2,1)} %bitcast.334) | data formatting | bytes 8388608 | tf_op jit(solution)/shard_map/reshape | solution.py:14
  271.3 53.9 %all-gather.8.cloned.1.call-done = bf16[2048,512]{1,0:T(8,128)(2,1)} async-done(((bf16[32,512]{1,0:T(8,128)(2,1)}), bf16[2048,512]{1,0:T(8,128)(2,1)}) %all-gather.8.cloned.1.call-update) | async-done | bytes 2097168 | tf_op jit(solution)/shard_map/all_gather | solution.py:95
  325.2 6.5 %fusion = f32[512,4,2,128]{3,0,2,1:T(8,128)} fusion(bf16[4,2,128,2048]{3,2,1,0:T(8,128)(2,1)} %bitcast.392, bf16[2048,512]{1,0:T(8,128)(2,1)} %all-gather.8.cloned.1.call-done), kind=kOutput, calls=%fused_computation.6 | convolution fusion | flops 2147483648 | bytes 8388608 | tf_op jit(solution)/shard_map/dot_general | solution.py:40
  332.9 71.8 %all-gather.4.cloned.1.call-done = bf16[2,2048,512]{2,1,0:T(8,128)(2,1)} async-done(((bf16[2,32,512]{2,1,0:T(8,128)(2,1)}), bf16[2,2048,512]{2,1,0:T(8,128)(2,1)}) %all-gather.4.cloned.1.call-update) | async-done | bytes 4194320 | tf_op jit(solution)/shard_map/all_gather | solution.py:94
  404.7 3.0 fusion.10
  419.2 62.6 %all-gather.6.cloned.1.call-done = bf16[64,28,512]{2,1,0:T(8,128)(2,1)} async-done(((bf16[1,28,512]{2,1,0:T(8,128)(2,1)}), bf16[64,28,512]{2,1,0:T(8,128)(2,1)}) %all-gather.6.cloned.1.call-update) | async-done | bytes 1835024 | tf_op jit(solution)/shard_map/all_gather | solution.py:154
  491.5 4.3 all-to-all-start.2
  521.0 4.2 all-to-all-start.3
  527.8 4.5 all-to-all-done.3
  (308 shorter events, 121.8 us)
Async XLA Ops:
  7.2 7.5 %copy-start.44 = (f32[2,512,32]{1,2,0:T(8,128)S(1)}, f32[2,512,32]{1,2,0:T(8,128)}, u32[]{:S(2)}) copy-start(f32[2,512,32]{1,2,0:T(8,128)} %param.12) | copy-start | bytes 393220
  9.8 65.4 %all-to-all-start = ((bf16[4,96,512]{2,1,0:T(8,128)(2,1)}), bf16[4,96,512]{2,1,0:T(8,128)(2,1)}, u32[]{:S(2)}, u32[]{:S(2)}) async-start(bf16[4,96,512]{2,1,0:T(8,128)(2,1)} %broadcast_in_dim.18), calls=%async_computation | async-start | bytes 786432 | tf_op jit(solution)/shard_map/all_to_all | solution.py:45
  14.7 226.2 %reduce-scatter.2.cloned.1.call-start = ((), (), s32[]{:S(2)}) async-start(), calls=%async_computation.6 | async-start | bytes 4259840 | tf_op jit(solution)/shard_map/reduce_scatter | solution.py:150
  14.7 59.9 %copy-start.41 = (bf16[2,32,512]{2,1,0:T(8,128)(2,1)}, bf16[2,32,512]{2,1,0:T(8,128)(2,1)S(1)}, u32[]{:S(2)}) copy-start(bf16[2,32,512]{2,1,0:T(8,128)(2,1)S(1)} %convert_bitcast_fusion.5) | copy-start | bytes 196612
  18.9 33.5 %copy-start.1 = (f32[512,1,1,128]{3,2,1,0:T(1,128)}, f32[512,1,1,128]{3,2,1,0:T(1,128)S(1)}, u32[]{:S(2)}) copy-start(f32[512,1,1,128]{3,2,1,0:T(1,128)S(1)} %get-tuple-element.63) | copy-start | bytes 786436
  19.0 33.5 %copy-start.3 = (f32[512,1,1,128]{3,2,1,0:T(1,128)}, f32[512,1,1,128]{3,2,1,0:T(1,128)S(1)}, u32[]{:S(2)}) copy-start(f32[512,1,1,128]{3,2,1,0:T(1,128)S(1)} %get-tuple-element.60) | copy-start | bytes 786436
  19.0 33.5 %copy-start.5 = (f32[512,1,1,128]{3,2,1,0:T(1,128)}, f32[512,1,1,128]{3,2,1,0:T(1,128)S(1)}, u32[]{:S(2)}) copy-start(f32[512,1,1,128]{3,2,1,0:T(1,128)S(1)} %get-tuple-element.64) | copy-start | bytes 786436
  44.1 17.3 %copy-start.58 = (s32[2,128]{1,0:T(2,128)S(1)}, s32[2,128]{1,0:T(2,128)}, u32[]{:S(2)}) copy-start(s32[2,128]{1,0:T(2,128)} %param.15) | copy-start | bytes 3076
  44.1 17.4 %copy-start.26 = (bf16[2,128,128]{2,1,0:T(8,128)(2,1)S(1)}, bf16[2,128,128]{2,1,0:T(8,128)(2,1)}, u32[]{:S(2)}) copy-start(bf16[2,128,128]{2,1,0:T(8,128)(2,1)} %param.21) | copy-start | bytes 196612
  97.7 227.5 %all-gather.8.cloned.1.call-start = ((), (), s32[]{:S(2)}) async-start(), calls=%async_computation.8 | async-start | bytes 2129920 | tf_op jit(solution)/shard_map/all_gather | solution.py:95
  99.2 305.4 %all-gather.4.cloned.1.call-start = ((), (), s32[]{:S(2)}) async-start(), calls=%async_computation.5 | async-start | bytes 4259840 | tf_op jit(solution)/shard_map/all_gather | solution.py:94
  105.8 40.7 %collective-permute-start = (bf16[512,1024]{1,0:T(8,128)(2,1)}, bf16[512,1024]{1,0:T(8,128)(2,1)}, u32[]{:S(2)}, u32[]{:S(2)}) collective-permute-start(bf16[512,1024]{1,0:T(8,128)(2,1)} %reshape.553), channel_id=1, source_target_pairs={{0,1},{1,2},{2,3},{3,0},{4,5},{5,6},{6,7},{7,4},{8,9},{9,10},{10,1... | collective-permute-start | bytes 3145736 | tf_op jit(solution)/shard_map/ppermute | solution.py:25
  107.3 42.2 %collective-permute-start.2 = (bf16[512,1024]{1,0:T(8,128)(2,1)}, bf16[512,1024]{1,0:T(8,128)(2,1)}, u32[]{:S(2)}, u32[]{:S(2)}) collective-permute-start(bf16[512,1024]{1,0:T(8,128)(2,1)} %reshape.553), channel_id=1, source_target_pairs={{1,0},{2,1},{3,2},{0,3},{5,4},{6,5},{7,6},{4,7},{9,8},{10,9},{11,1... | collective-permute-start | bytes 3145736 | tf_op jit(solution)/shard_map/ppermute | solution.py:28
  144.9 24.6 %copy-start.11 = (bf16[1,512,1024]{2,1,0:T(8,128)(2,1)S(1)}, bf16[1,512,1024]{2,1,0:T(8,128)(2,1)}, u32[]{:S(2)}) copy-start(bf16[1,512,1024]{2,1,0:T(8,128)(2,1)} %stack_reshape.3) | copy-start | bytes 3145732
  146.5 23.0 %collective-permute-start.1 = (bf16[512,1024]{1,0:T(8,128)(2,1)}, bf16[512,1024]{1,0:T(8,128)(2,1)S(1)}, u32[]{:S(2)}, u32[]{:S(2)}) collective-permute-start(bf16[512,1024]{1,0:T(8,128)(2,1)} %collective-permute-done), channel_id=1, source_target_pairs={{0,1},{1,2},{2,3},{3,0},{4,5},{5,6},{6,7},{7,4},{8,9},{9,10},{10,1... | collective-permute-start | bytes 3145736 | tf_op jit(solution)/shard_map/ppermute | solution.py:25
  242.2 28.5 %all-to-all-start.1 = ((f32[4,4,512]{2,1,0:T(4,128)}), f32[4,4,512]{2,1,0:T(4,128)S(1)}, u32[]{:S(2)}, u32[]{:S(2)}) async-start(f32[4,4,512]{2,1,0:T(4,128)} %broadcast_in_dim.20), calls=%async_computation.2 | async-start | bytes 65536 | tf_op jit(solution)/shard_map/all_to_all | solution.py:45
  246.1 235.7 %all-gather.6.cloned.1.call-start = ((), (), s32[]{:S(2)}) async-start(), calls=%async_computation.7 | async-start | bytes 2129920 | tf_op jit(solution)/shard_map/all_gather | solution.py:154
  418.1 64.9 %copy-start.71 = (s32[32]{0:T(128)S(1)}, s32[32]{0:T(128)}, u32[]{:S(2)}) copy-start(s32[32]{0:T(128)} %copy-done.70) | copy-start | bytes 388
  419.2 66.5 %copy-start.59 = (s32[2,128]{1,0:T(2,128)S(1)}, s32[2,128]{1,0:T(2,128)}, u32[]{:S(2)}) copy-start(s32[2,128]{1,0:T(2,128)} %param.15) | copy-start | bytes 3076
  487.4 12.0 %copy-start.66 = (s32[512]{0:T(512)S(1)}, s32[512]{0:T(512)}, u32[]{:S(2)}) copy-start(s32[512]{0:T(512)} %copy-done.65) | copy-start | bytes 6148
  491.5 28.7 %all-to-all-start.2 = ((bf16[4,96,512]{2,1,0:T(8,128)(2,1)}), bf16[4,96,512]{2,1,0:T(8,128)(2,1)}, u32[]{:S(2)}, u32[]{:S(2)}) async-start(bf16[4,96,512]{2,1,0:T(8,128)(2,1)} %broadcast_in_dim.21), calls=%async_computation.3 | async-start | bytes 786432 | tf_op jit(solution)/shard_map/all_to_all | solution.py:45
  518.0 14.3 %copy-start.16 = (bf16[256,512]{1,0:T(8,128)(2,1)S(1)}, bf16[256,512]{1,0:T(8,128)(2,1)}, u32[]{:S(2)}) copy-start(bf16[256,512]{1,0:T(8,128)(2,1)} %copy-done.14) | copy-start | bytes 786436
  519.4 13.3 %copy-start.8 = (bf16[512,512]{1,0:T(8,128)(2,1)S(1)}, bf16[512,512]{1,0:T(8,128)(2,1)}, u32[]{:S(2)}) copy-start(bf16[512,512]{1,0:T(8,128)(2,1)} %copy-done.7) | copy-start | bytes 1572868
  521.0 11.2 %all-to-all-start.3 = ((bf16[4,96,512]{2,1,0:T(8,128)(2,1)}), bf16[4,96,512]{2,1,0:T(8,128)(2,1)S(1)}, u32[]{:S(2)}, u32[]{:S(2)}) async-start(bf16[4,96,512]{2,1,0:T(8,128)(2,1)} %broadcast_in_dim.26), calls=%async_computation.4 | async-start | bytes 786432 | tf_op jit(solution)/shard_map/all_to_all | solution.py:45
  (68 other events, 216.8 us)
Sparse Core Ops, SparseCore 0:
  97.8 142.9 reduce-scatter.1
  243.6 81.5 all-gather.7
  328.0 76.6 all-gather.3
  407.3 74.4 all-gather.5
